TPU v7x, 128 devices: a whole 4x4x4 slice. The times are simulated.
128 devices in a mesh: fsdp: 128 (over z, y, x, core).
Axes of the slice: x: 4, y: 4, z: 4, core: 2. Of those that a mesh axis runs over, the one named last changes fastest.
Arguments:
- x: bfloat16 [512, 512, 512], P('fsdp')
- lengths: int32 [512], P('fsdp')
- d_y: bfloat16 [512, 512, 512], P('fsdp')
- w_attn: bfloat16 [2, 4, 512, 512], P(None, None, 'fsdp')
- b_attn: bfloat16 [2, 4, 512], P(None, None, 'fsdp')
- ln_par: bfloat16 [2, 4, 512], P(None, None, 'fsdp')
- w_up: bfloat16 [2, 512, 2048], P(None, 'fsdp')
- b_up: bfloat16 [2, 2048], P(None, 'fsdp')
- w_down: bfloat16 [2, 2048, 512], P(None, 'fsdp')
- b_down: bfloat16 [2, 512], P(None, 'fsdp')
Outputs:
- output 1: bfloat16 [512, 512, 512], P('fsdp')
- output 2: float32 [2, 4, 512, 512], P(None, None, 'fsdp')
- output 3: float32 [2, 4, 512], P(None, None, 'fsdp')
- output 4: float32 [2, 4, 512], P(None, None, 'fsdp')
- output 5: float32 [2, 512, 2048], P(None, 'fsdp')
- output 6: float32 [2, 2048], P(None, 'fsdp')
- output 7: float32 [2, 2048, 512], P(None, 'fsdp')
- output 8: float32 [2, 512], P(None, 'fsdp')
All inputs are finite; a program needn't handle non-finite values.
Results may differ from a plain program's by a relative error of at most 0.0133484.
Values are sent between devices in bfloat16 or wider.
A program may use at most 1 GiB of HBM per device.

v0:
```python
import math
import functools
import jax
import jax.numpy as jnp
from jax import lax
from jax.sharding import PartitionSpec as P

HEAD_DIM = 64
EPS = 1e-5
THETA = 10000.0
NEG_BIG = -1e30


def rotary_tables(seq_len):
    half_dim = HEAD_DIM // 2
    inv_freq = 1.0 / (THETA ** (jnp.arange(half_dim, dtype=jnp.float32) * (2.0 / HEAD_DIM)))
    angles = jnp.arange(seq_len, dtype=jnp.float32)[:, None] * inv_freq[None, :]
    return jnp.cos(angles)[:, None, :], jnp.sin(angles)[:, None, :]


def rotate(tensor, cos_tab, sin_tab):
    half_dim = HEAD_DIM // 2
    first_half = tensor[..., :half_dim]
    second_half = tensor[..., half_dim:]
    return jnp.concatenate([first_half * cos_tab - second_half * sin_tab, second_half * cos_tab + first_half * sin_tab], axis=-1)


def rotate_back(tensor, cos_tab, sin_tab):
    half_dim = HEAD_DIM // 2
    first_half = tensor[..., :half_dim]
    second_half = tensor[..., half_dim:]
    return jnp.concatenate([first_half * cos_tab + second_half * sin_tab, second_half * cos_tab - first_half * sin_tab], axis=-1)


def norm_fwd(x_in, gain, shift):
    row_mean = jnp.mean(x_in, axis=-1, keepdims=True)
    centered = x_in - row_mean
    variance = jnp.mean(centered * centered, axis=-1, keepdims=True)
    return centered * lax.rsqrt(variance + EPS) * gain + shift


def gelu_slope(pre_act):
    normal_cdf = 0.5 * (1.0 + lax.erf(pre_act * (1.0 / math.sqrt(2.0))))
    density = jnp.exp(-0.5 * pre_act * pre_act) * (1.0 / math.sqrt(2.0 * math.pi))
    return normal_cdf + pre_act * density


def layer_forward(x, weights, lengths, tables):
    w_attn, b_attn, ln_par, w_up, b_up, w_down, b_down = weights
    cos_tab, sin_tab = tables
    num_seq, seq_len, model_dim = x.shape
    num_heads = model_dim // HEAD_DIM
    x_f32 = x.astype(jnp.float32)
    h_one = norm_fwd(x_f32, ln_par[0].astype(jnp.float32), ln_par[1].astype(jnp.float32)).astype(jnp.bfloat16)
    projected = jnp.einsum('bld,kde->kble', h_one, w_attn[:3], preferred_element_type=jnp.float32)
    projected = (projected + b_attn[:3, None, None, :].astype(jnp.float32)).reshape(3, num_seq, seq_len, num_heads, HEAD_DIM)
    query_rot = rotate(projected[0] * (HEAD_DIM ** -0.5), cos_tab, sin_tab).astype(jnp.bfloat16)
    key_rot = rotate(projected[1], cos_tab, sin_tab).astype(jnp.bfloat16)
    values = projected[2].astype(jnp.bfloat16)
    scores = jnp.einsum('bqhd,bkhd->bhqk', query_rot, key_rot, preferred_element_type=jnp.float32)
    key_valid = jnp.arange(seq_len)[None, None, None, :] < lengths[:, None, None, None]
    probs_bf = jax.nn.softmax(jnp.where(key_valid, scores, NEG_BIG), axis=-1).astype(jnp.bfloat16)
    context = jnp.einsum('bhqk,bkhd->bqhd', probs_bf, values, preferred_element_type=jnp.float32)
    context = context.astype(jnp.bfloat16).reshape(num_seq, seq_len, model_dim)
    attn_out = jnp.einsum('bld,de->ble', context, w_attn[3], preferred_element_type=jnp.float32)
    x_mid = (x_f32 + attn_out + b_attn[3].astype(jnp.float32)).astype(jnp.bfloat16)
    mid_f32 = x_mid.astype(jnp.float32)
    h_two = norm_fwd(mid_f32, ln_par[2].astype(jnp.float32), ln_par[3].astype(jnp.float32)).astype(jnp.bfloat16)
    pre_act = jnp.einsum('bld,df->blf', h_two, w_up, preferred_element_type=jnp.float32) + b_up.astype(jnp.float32)
    act_bf = jax.nn.gelu(pre_act, approximate=False).astype(jnp.bfloat16)
    mlp_out = jnp.einsum('blf,fd->bld', act_bf, w_down, preferred_element_type=jnp.float32)
    y_out = (mid_f32 + mlp_out + b_down.astype(jnp.float32)).astype(jnp.bfloat16)
    saved_acts = (x, h_one, query_rot, key_rot, values, probs_bf, context, x_mid, h_two, pre_act, act_bf)
    return y_out, saved_acts


def layer_backward(d_out, saved_acts, weights, tables):
    w_attn, ln_par, w_up, w_down = weights[0], weights[2], weights[3], weights[5]
    cos_tab, sin_tab = tables
    x, h_one, query_rot, key_rot, values, probs_bf, context, x_mid, h_two, pre_act, act_bf = saved_acts
    num_seq, seq_len, model_dim = x.shape
    num_heads = model_dim // HEAD_DIM
    gb_down = jnp.sum(d_out, axis=(0, 1), dtype=jnp.float32)
    gw_down = jnp.einsum('blf,bld->fd', act_bf, d_out, preferred_element_type=jnp.float32)
    d_act = jnp.einsum('bld,fd->blf', d_out, w_down, preferred_element_type=jnp.float32)
    d_pre = d_act * gelu_slope(pre_act)
    gb_up = jnp.sum(d_pre, axis=(0, 1))
    d_pre_bf = d_pre.astype(jnp.bfloat16)
    gw_up = jnp.einsum('bld,blf->df', h_two, d_pre_bf, preferred_element_type=jnp.float32)
    d_h_two = jnp.einsum('blf,df->bld', d_pre_bf, w_up, preferred_element_type=jnp.float32)
    _, norm_pull_two = jax.vjp(norm_fwd, x_mid.astype(jnp.float32), ln_par[2].astype(jnp.float32), ln_par[3].astype(jnp.float32))
    d_mid_norm, g_gain_two, g_shift_two = norm_pull_two(d_h_two)
    d_mid = (d_out.astype(jnp.float32) + d_mid_norm).astype(jnp.bfloat16)
    gb_out = jnp.sum(d_mid, axis=(0, 1), dtype=jnp.float32)
    gw_out = jnp.einsum('bld,ble->de', context, d_mid, preferred_element_type=jnp.float32)
    d_context = jnp.einsum('ble,de->bld', d_mid, w_attn[3], preferred_element_type=jnp.float32)
    d_context = d_context.astype(jnp.bfloat16).reshape(num_seq, seq_len, num_heads, HEAD_DIM)
    d_probs = jnp.einsum('bqhd,bkhd->bhqk', d_context, values, preferred_element_type=jnp.float32)
    d_values = jnp.einsum('bhqk,bqhd->bkhd', probs_bf, d_context, preferred_element_type=jnp.float32)
    probs_f32 = probs_bf.astype(jnp.float32)
    d_scores = (probs_f32 * (d_probs - jnp.sum(d_probs * probs_f32, axis=-1, keepdims=True))).astype(jnp.bfloat16)
    d_query = jnp.einsum('bhqk,bkhd->bqhd', d_scores, key_rot, preferred_element_type=jnp.float32)
    d_key = jnp.einsum('bhqk,bqhd->bkhd', d_scores, query_rot, preferred_element_type=jnp.float32)
    d_proj = jnp.stack([
        (rotate_back(d_query, cos_tab, sin_tab) * (HEAD_DIM ** -0.5)).astype(jnp.bfloat16),
        rotate_back(d_key, cos_tab, sin_tab).astype(jnp.bfloat16),
        d_values.astype(jnp.bfloat16)]).reshape(3, num_seq, seq_len, model_dim)
    gb_qkv = jnp.sum(d_proj, axis=(1, 2), dtype=jnp.float32)
    gw_qkv = jnp.einsum('bld,kble->kde', h_one, d_proj, preferred_element_type=jnp.float32)
    d_h_one = jnp.einsum('kble,kde->bld', d_proj, w_attn[:3], preferred_element_type=jnp.float32)
    _, norm_pull_one = jax.vjp(norm_fwd, x.astype(jnp.float32), ln_par[0].astype(jnp.float32), ln_par[1].astype(jnp.float32))
    d_x_norm, g_gain_one, g_shift_one = norm_pull_one(d_h_one)
    d_x = (d_mid.astype(jnp.float32) + d_x_norm).astype(jnp.bfloat16)
    gb_attn = jnp.concatenate([gb_qkv, gb_out[None]], axis=0)
    g_ln = jnp.stack([g_gain_one, g_shift_one, g_gain_two, g_shift_two])
    return d_x, (gw_qkv, gw_out, gb_attn, g_ln, gw_up, gb_up, gw_down, gb_down)


def gather_layer(layer_shards, axis_name):
    w_attn, b_attn, ln_par, w_up, b_up, w_down, b_down = layer_shards
    return (lax.all_gather(w_attn, axis_name, axis=1, tiled=True),
            lax.all_gather(b_attn, axis_name, axis=1, tiled=True),
            lax.all_gather(ln_par, axis_name, axis=1, tiled=True),
            lax.all_gather(w_up, axis_name, axis=0, tiled=True),
            lax.all_gather(b_up, axis_name, axis=0, tiled=True),
            lax.all_gather(w_down, axis_name, axis=0, tiled=True),
            lax.all_gather(b_down, axis_name, axis=0, tiled=True))


def scatter_grads(layer_grads, axis_name):
    gw_qkv, gw_out, gb_attn, g_ln, gw_up, gb_up, gw_down, gb_down = layer_grads
    reduce_rows = functools.partial(lax.psum_scatter, axis_name=axis_name, tiled=True)
    attn_part = jnp.concatenate([reduce_rows(gw_qkv, scatter_dimension=1), reduce_rows(gw_out, scatter_dimension=0)[None]], axis=0)
    return (attn_part,
            reduce_rows(gb_attn, scatter_dimension=1),
            reduce_rows(g_ln, scatter_dimension=1),
            reduce_rows(gw_up, scatter_dimension=0),
            reduce_rows(gb_up, scatter_dimension=0),
            reduce_rows(gw_down, scatter_dimension=0),
            reduce_rows(gb_down, scatter_dimension=0))


def solution(mesh):
    axis_name = mesh.axis_names[0]
    batch_spec = P(axis_name)
    weight_specs = (P(None, None, axis_name, None), P(None, None, axis_name), P(None, None, axis_name),
                    P(None, axis_name, None), P(None, axis_name), P(None, axis_name, None), P(None, axis_name))

    def device_step(x, lengths, d_y, w_attn, b_attn, ln_par, w_up, b_up, w_down, b_down):
        shards = (w_attn, b_attn, ln_par, w_up, b_up, w_down, b_down)
        num_layers = w_attn.shape[0]
        tables = rotary_tables(x.shape[1])
        hidden = x
        saved_list = []
        for layer_idx in range(num_layers):
            full_wts = gather_layer(tuple(shard[layer_idx] for shard in shards), axis_name)
            hidden, saved_acts = layer_forward(hidden, full_wts, lengths, tables)
            saved_list.append(saved_acts)
        grad_x = d_y
        grads_list = [None] * num_layers
        for layer_idx in reversed(range(num_layers)):
            layer_shards, grad_x = lax.optimization_barrier((tuple(shard[layer_idx] for shard in shards), grad_x))
            full_wts = gather_layer(layer_shards, axis_name)
            grad_x, layer_grads = layer_backward(grad_x, saved_list[layer_idx], full_wts, tables)
            grads_list[layer_idx] = scatter_grads(layer_grads, axis_name)
        stacked = tuple(jnp.stack([grads_list[layer_pos][field_pos] for layer_pos in range(num_layers)]) for field_pos in range(7))
        return (grad_x,) + stacked

    return jax.shard_map(device_step, mesh=mesh,
                         in_specs=(batch_spec, batch_spec, batch_spec) + weight_specs,
                         out_specs=(batch_spec,) + weight_specs,
                         check_vma=False)
```

profile of v0, /device:TPU:1, one launch (start us, length us, event | category | flops | bytes accessed | tf_op | source)
XLA Modules:
  0.0 2430.4 jit_solution(18163868751641950328)
XLA Ops:
  17.3 38.9 %all-gather.2 = bf16[1,4,512]{1,0,2:T(2,128)(2,1)S(1)} all-gather(bf16[1,4,4]{1,0,2:T(2,128)(2,1)S(1)} %copy.344), channel_id=4, replica_groups=mesh['fsdp'=128] {'fsdp'}, dimensions={2}, use_global_device_ids=true | all-gather | bytes 4128 | tf_op jit(solution)/shard_map/all_gather | solution.py:122
  60.4 33.3 %all-gather.9 = bf16[1,4,512]{1,0,2:T(2,128)(2,1)S(1)} all-gather(bf16[1,4,4]{1,0,2:T(2,128)(2,1)S(1)} %copy.347), channel_id=11, replica_groups=mesh['fsdp'=128] {'fsdp'}, dimensions={2}, use_global_device_ids=true | all-gather | bytes 4128 | tf_op jit(solution)/shard_map/all_gather | solution.py:122
  101.2 64.2 %all-reduce.19 = (bf16[512]{0:T(512)(128)(2,1)S(1)}, bf16[2048]{0:T(1024)(128)(2,1)S(1)}, bf16[2048]{0:T(1024)(128)(2,1)S(1)}) all-reduce(bf16[512]{0:T(512)(128)(2,1)S(1)} %dynamic-update-slice.1, bf16[2048]{0:T(1024)(128)(2,1)S(1)} %dynamic-update-slice, bf16[2048]{0:T(1024)(128)(2,1)S(1)} %dynamic-update-slice.2), channel_id=8, replica_groups=mesh['fsdp'=128] {'fsdp'}, use_global_device_ids=true, to_apply=%add.1 | all-reduce | flops 4608 | bytes 18432
  166.4 34.1 %all-gather.13 = bf16[128,4,4]{2,1,0:T(4,128)(2,1)S(1)} all-gather(bf16[1,4,4]{2,1,0:T(4,128)(2,1)S(1)} %bitcast.351), channel_id=1, replica_groups=mesh['fsdp'=128] {'fsdp'}, dimensions={0}, use_global_device_ids=true | all-gather | bytes 4128 | tf_op jit(solution)/shard_map/all_gather | solution.py:123
  201.8 33.9 %all-gather = bf16[1,4,512]{1,0,2:T(2,128)(2,1)S(1)} all-gather(bf16[1,4,4]{1,0,2:T(2,128)(2,1)S(1)} %copy.339), channel_id=2, replica_groups=mesh['fsdp'=128] {'fsdp'}, dimensions={2}, use_global_device_ids=true | all-gather | bytes 4128 | tf_op jit(solution)/shard_map/all_gather | solution.py:123
  242.9 33.5 %all-gather.7 = bf16[1,4,512]{1,0,2:T(2,128)(2,1)S(1)} all-gather(bf16[1,4,4]{1,0,2:T(2,128)(2,1)S(1)} %copy.341), channel_id=9, replica_groups=mesh['fsdp'=128] {'fsdp'}, dimensions={2}, use_global_device_ids=true | all-gather | bytes 4128 | tf_op jit(solution)/shard_map/all_gather | solution.py:123
  322.6 19.7 fusion.239
  342.3 12.4 divide_convert_fusion.1
  366.1 18.1 fusion.112
  384.3 40.7 %fusion.14 = bf16[4,512,2048]{2,1,0:T(8,128)(2,1)} fusion(f32[4,512,2048]{2,1,0:T(8,128)} %get-tuple-element.162, f32[2048]{0:T(1024)S(1)} %convert_element_type.463, u8[512,2048]{1,0:T(8,128)(4,1)S(1)} %get-tuple-element.63, u8[512,2048]{1,0:T(8,128)(4,1)S(1)} %get-tuple-element.62), kind=kLoop, calls=%fused_computation.24 | loop fusion | flops 297795584 | bytes 27271168 | tf_op jit(solution)/shard_map/convert_element_type | solution.py:70
  456.3 19.4 fusion.240
  475.7 12.8 divide_convert_fusion
  500.7 18.7 fusion.113
  519.4 16.6 fusion.245
  539.9 11.1 fusion.241
  574.5 12.9 convolution_convert_fusion.3
  587.4 17.7 fusion.2
  605.2 27.7 %fusion.3 = bf16[4,8,512,512]{2,3,1,0:T(8,128)(2,1)} fusion(f32[4,8,512,512]{2,3,1,0:T(8,128)} %get-tuple-element.170, f32[4,8,512]{2,1,0:T(8,128)S(1)} %get-tuple-element.169, f32[4,8,512,512]{2,3,1,0:T(8,128)} %get-tuple-element.166, f32[4,8,512]{2,1,0:T(8,128)S(1)} %get-tuple-element.165), kind=kLoop, calls=%fused_computation.7 | loop fusion | flops 50331648 | bytes 84017152 | tf_op jit(solution)/shard_map/convert_element_type | solution.py:101
  632.8 13.6 convolution_bitcast_fusion.5
  646.4 11.1 convolution_bitcast_fusion.6
  706.4 45.2 %fusion.124 = f32[2048,512]{1,0:T(8,128)} fusion(bf16[4,512,512]{2,1,0:T(8,128)(2,1)} %param.12, f32[4,512,2048]{2,1,0:T(8,128)} %get-tuple-element.185, f32[2048]{0:T(1024)S(1)} %copy-done.79, u8[512,2048]{1,0:T(8,128)(4,1)} %get-tuple-element.61, u8[512,2048]{1,0:T(8,128)(4,1)S(1)} %copy-done.104), kind=kOutput, calls=%fused_computation.186 | convolution fusion | flops 4592762880 | bytes 25174016 | tf_op jit(solution)/shard_map/blf,bld->fd/dot_general | solution.py:84
  765.9 33.4 %all-gather.15 = bf16[128,4,4]{2,1,0:T(4,128)(2,1)S(1)} all-gather(bf16[1,4,4]{2,1,0:T(4,128)(2,1)S(1)} %bitcast.352), channel_id=1, replica_groups=mesh['fsdp'=128] {'fsdp'}, dimensions={0}, use_global_device_ids=true | all-gather | bytes 4128 | tf_op jit(solution)/shard_map/all_gather | solution.py:123
  833.1 13.4 fusion.246
  867.2 31.8 %all-gather.34.cloned.1.call-done = bf16[4,512,512]{2,0,1:T(4,128)(2,1)} async-done(((bf16[4,4,512]{2,0,1:T(4,128)(2,1)}), bf16[4,512,512]{2,0,1:T(4,128)(2,1)}) %all-gather.34.cloned.1.call-update) | async-done | bytes 2097168 | tf_op jit(solution)/shard_map/all_gather | solution.py:121
  906.0 13.0 convolution_convert_fusion.2
  919.0 17.1 fusion.4
  940.4 27.9 %fusion.5 = bf16[4,8,512,512]{2,3,1,0:T(8,128)(2,1)} fusion(f32[4,8,512,512]{2,3,1,0:T(8,128)} %get-tuple-element.172, f32[4,8,512]{2,1,0:T(8,128)S(1)} %get-tuple-element.171, f32[4,8,512,512]{2,3,1,0:T(8,128)} %get-tuple-element.159, f32[4,8,512]{2,1,0:T(8,128)S(1)} %copy-done.49), kind=kLoop, calls=%fused_computation.9 | loop fusion | flops 50331648 | bytes 84017152 | tf_op jit(solution)/shard_map/convert_element_type | solution.py:101
  968.4 13.3 convolution_bitcast_fusion.2
  1064.2 64.4 %all-reduce.17 = (f32[4,512]{1,0:T(4,128)S(1)}, f32[4,512]{1,0:T(4,128)S(1)}, f32[4,512]{1,0:T(4,128)S(1)}, f32[4,512]{1,0:T(4,128)S(1)}, f32[2048]{0:T(1024)S(1...) all-reduce(f32[4,512]{1,0:T(4,128)S(1)} %pad_maximum_fusion.36, ...), channel_id=19, replica_groups=mesh['fsdp'=128] {'fsdp'}, use_global_device_ids=true, to_apply=%region_31.32.clone | all-reduce | flops 13312 | bytes 106496
  1131.3 411.0 %reduce-scatter.11.cloned.1.call-done = f32[16,512]{1,0:T(8,128)} async-done(((f32[2048,512]{1,0:T(8,128)}), f32[16,512]{1,0:T(8,128)}) %reduce-scatter.11.cloned.1.call-update) | async-done | bytes 32784 | tf_op jit(solution)/shard_map/reduce_scatter | solution.py:139
  1542.3 646.7 %reduce-scatter.9.cloned.1.call-done = f32[16,512]{1,0:T(8,128)} async-done(((f32[2048,512]{1,0:T(8,128)}), f32[16,512]{1,0:T(8,128)}) %reduce-scatter.9.cloned.1.call-update) | async-done | bytes 32784 | tf_op jit(solution)/shard_map/reduce_scatter | solution.py:139
  2190.4 228.5 %all-reduce.22.cloned.1.call-done = (f32[512,512]{0,1:T(8,128)}, f32[3,512,512]{2,0,1:T(4,128)}, f32[512,512]{0,1:T(8,128)}, f32[3,512,512]{2,0,1:T(4,128)}, f32[512,2048]{1,0:T(8,128)}, /*index=5*/f32[512,2048]{1,0:T(8,128)}) async-done(((f32[512,512]{0,1:T(8,128)}, f32[3,512,512]{2,0,1:T(4,128)}, f32[512,512]{0,1:T(8,128)}, f32[3,512,512]{2,0,1:T(4,128)}, f32[512,2048]{1,0:T(8,128)}, ...) | async-done | bytes 16777232
  (410 shorter events, 378.3 us)
Async XLA Ops:
  7.2 285.0 %all-gather.36.cloned.1.call-start = ((), (), s32[]{:S(2)}) async-start(), calls=%async_computation.8 | async-start | bytes 2113536 | tf_op jit(solution)/shard_map/all_gather | solution.py:121
  8.6 303.2 %all-gather.42.cloned.1.call-start = ((), (), s32[]{:S(2)}) async-start(), calls=%async_computation.11 | async-start | bytes 2113536 | tf_op jit(solution)/shard_map/all_gather | solution.py:121
  9.3 356.8 %all-gather.38.cloned.1.call-start = ((), (), s32[]{:S(2)}) async-start(), calls=%async_computation.9 | async-start | bytes 4227072 | tf_op jit(solution)/shard_map/all_gather | solution.py:124
  11.4 413.7 %all-gather.40.cloned.1.call-start = ((), (), s32[]{:S(2)}) async-start(), calls=%async_computation.10 | async-start | bytes 2113536 | tf_op jit(solution)/shard_map/all_gather | solution.py:126
  12.8 487.9 %all-gather.44.cloned.1.call-start = ((), (), s32[]{:S(2)}) async-start(), calls=%async_computation.12 | async-start | bytes 4227072 | tf_op jit(solution)/shard_map/all_gather | solution.py:124
  13.5 505.9 %all-gather.28.cloned.1.call-start = ((), (), s32[]{:S(2)}) async-start(), calls=%async_computation.2 | async-start | bytes 2113536 | tf_op jit(solution)/shard_map/all_gather | solution.py:126
  14.9 521.1 %all-gather.46.cloned.1.call-start = ((), (), s32[]{:S(2)}) async-start(), calls=%async_computation.13 | async-start | bytes 2113536 | tf_op jit(solution)/shard_map/all_gather | solution.py:124
  15.6 552.0 %all-gather.30.cloned.1.call-start = ((), (), s32[]{:S(2)}) async-start(), calls=%async_computation.3 | async-start | bytes 2113536 | tf_op jit(solution)/shard_map/all_gather | solution.py:121
  16.4 805.3 %all-gather.48.cloned.1.call-start = ((), (), s32[]{:S(2)}) async-start(), calls=%async_computation.14 | async-start | bytes 2113536 | tf_op jit(solution)/shard_map/all_gather | solution.py:124
  165.7 218.6 %copy-start.72 = (f32[2048]{0:T(1024)}, f32[2048]{0:T(1024)S(1)}, u32[]{:S(2)}) copy-start(f32[2048]{0:T(1024)S(1)} %convert_element_type.463) | copy-start | bytes 24580
  201.6 248.8 %copy-start.40 = (f32[512,32]{0,1:T(8,128)}, f32[512,32]{0,1:T(8,128)S(1)}, u32[]{:S(2)}) copy-start(f32[512,32]{0,1:T(8,128)S(1)} %get-tuple-element.156) | copy-start | bytes 196612
  201.6 248.8 %copy-start.43 = (f32[512,32]{0,1:T(8,128)}, f32[512,32]{0,1:T(8,128)S(1)}, u32[]{:S(2)}) copy-start(f32[512,32]{0,1:T(8,128)S(1)} %get-tuple-element.157) | copy-start | bytes 196612
  242.8 53.5 %copy-start.88 = (f32[512]{0:T(512)}, f32[512]{0:T(512)S(1)}, u32[]{:S(2)}) copy-start(f32[512]{0:T(512)S(1)} %get-tuple-element.77) | copy-start | bytes 6148
  242.9 53.5 %copy-start.90 = (f32[512]{0:T(512)}, f32[512]{0:T(512)S(1)}, u32[]{:S(2)}) copy-start(f32[512]{0:T(512)S(1)} %get-tuple-element.78) | copy-start | bytes 6148
  242.9 123.3 %copy-start.84 = (f32[512]{0:T(512)}, f32[512]{0:T(512)S(1)}, u32[]{:S(2)}) copy-start(f32[512]{0:T(512)S(1)} %get-tuple-element.76) | copy-start | bytes 6148
  242.9 123.3 %copy-start.86 = (f32[512]{0:T(512)}, f32[512]{0:T(512)S(1)}, u32[]{:S(2)}) copy-start(f32[512]{0:T(512)S(1)} %get-tuple-element.79) | copy-start | bytes 6148
  284.1 150.5 %copy-start.96 = (f32[512]{0:T(512)}, f32[512]{0:T(512)S(1)}, u32[]{:S(2)}) copy-start(f32[512]{0:T(512)S(1)} %get-tuple-element.73) | copy-start | bytes 6148
  284.1 150.5 %copy-start.98 = (f32[512]{0:T(512)}, f32[512]{0:T(512)S(1)}, u32[]{:S(2)}) copy-start(f32[512]{0:T(512)S(1)} %get-tuple-element.74) | copy-start | bytes 6148
  287.1 74.2 %copy-start.2 = (bf16[4,512,512]{1,2,0:T(8,128)(2,1)}, bf16[4,512,512]{1,2,0:T(8,128)(2,1)S(1)}, u32[]{:S(2)}) copy-start(bf16[4,512,512]{1,2,0:T(8,128)(2,1)S(1)} %copy.217) | copy-start | bytes 6291460
  384.3 40.8 %copy-start.9 = (bf16[4,512,512]{1,2,0:T(8,128)(2,1)S(1)}, bf16[4,512,512]{1,2,0:T(8,128)(2,1)}, u32[]{:S(2)}) copy-start(bf16[4,512,512]{1,2,0:T(8,128)(2,1)} %copy-done.8) | copy-start | bytes 6291460
  498.8 64.5 %copy-start.56 = (f32[4,512]{1,0:T(4,128)}, f32[4,512]{1,0:T(4,128)S(1)}, u32[]{:S(2)}) copy-start(f32[4,512]{1,0:T(4,128)S(1)} %broadcast_multiply_fusion) | copy-start | bytes 24580
  500.7 62.6 %copy-start.70 = (f32[4,512]{1,0:T(4,128)}, f32[4,512]{1,0:T(4,128)S(1)}, u32[]{:S(2)}) copy-start(f32[4,512]{1,0:T(4,128)S(1)} %fusion.176) | copy-start | bytes 24580
  705.0 128.0 %all-gather.32.cloned.1.call-start = ((), (), s32[]{:S(2)}) async-start(), calls=%async_computation.4 | async-start | bytes 2113536 | tf_op jit(solution)/shard_map/all_gather | solution.py:126
  705.6 193.3 %all-gather.34.cloned.1.call-start = ((), (), s32[]{:S(2)}) async-start(), calls=%async_computation.5 | async-start | bytes 2113536 | tf_op jit(solution)/shard_map/all_gather | solution.py:121
  706.4 835.9 %reduce-scatter.11.cloned.1.call-start = ((), (), s32[]{:S(2)}) async-start(), calls=%async_computation.7 | async-start | bytes 4227072 | tf_op jit(solution)/shard_map/reduce_scatter | solution.py:139
  751.7 1437.3 %reduce-scatter.9.cloned.1.call-start = ((), (), s32[]{:S(2)}) async-start(), calls=%async_computation.6 | async-start | bytes 4227072 | tf_op jit(solution)/shard_map/reduce_scatter | solution.py:139
  765.7 38.9 %copy-start.16 = (bf16[4,512,512]{1,2,0:T(8,128)(2,1)S(1)}, bf16[4,512,512]{1,2,0:T(8,128)(2,1)}, u32[]{:S(2)}) copy-start(bf16[4,512,512]{1,2,0:T(8,128)(2,1)} %copy-done.14) | copy-start | bytes 6291460
  765.7 38.9 %copy-start.57 = (f32[4,512]{1,0:T(4,128)S(1)}, f32[4,512]{1,0:T(4,128)}, u32[]{:S(2)}) copy-start(f32[4,512]{1,0:T(4,128)} %copy-done.56) | copy-start | bytes 24580
  765.7 38.9 %copy-start.71 = (f32[4,512]{1,0:T(4,128)S(1)}, f32[4,512]{1,0:T(4,128)}, u32[]{:S(2)}) copy-start(f32[4,512]{1,0:T(4,128)} %copy-done.70) | copy-start | bytes 24580
  765.7 38.9 %copy-start.93 = (f32[512]{0:T(512)S(1)}, f32[512]{0:T(512)}, u32[]{:S(2)}) copy-start(f32[512]{0:T(512)} %get-tuple-element.72) | copy-start | bytes 6148
  765.8 38.9 %copy-start.95 = (f32[512]{0:T(512)S(1)}, f32[512]{0:T(512)}, u32[]{:S(2)}) copy-start(f32[512]{0:T(512)} %get-tuple-element.75) | copy-start | bytes 6148
  821.2 1597.7 %all-reduce.22.cloned.1.call-start = ((), (), s32[]{:S(2)}) async-start(), calls=%async_computation.15 | async-start | bytes 37748736
  (89 other events, 658.6 us)
Sparse Core Ops, SparseCore 0:
  11.1 68.9 all-gather.35
  83.2 62.7 all-gather.41
  149.2 64.1 all-gather.37
  216.3 62.7 all-gather.39
  282.2 64.0 all-gather.43
  349.2 62.7 all-gather.27
  415.1 62.7 all-gather.45
  481.0 62.7 all-gather.29
  705.2 62.0 all-gather.47
  770.3 62.7 all-gather.31
  836.2 62.7 all-gather.33
  901.2 641.0 reduce-scatter.10
  1544.6 644.3 reduce-scatter.8
  2195.3 223.5 all-reduce.21
where the time goes:
time: 2440 us; the launch traced here: 2430 us
  waiting for transfers between devices  1330 us (55%)
  matrix products  390 us (16%)
  blocking collectives  336 us (14%)
  other arithmetic  237 us (10%)
  local copies, waits for them, and re-layouts  122 us (5%)
    reduce_scatter x2, waiting for transfers between devices, scatter_grads(): reduce_rows(gw_down, scatter_dimension=0)  1060 us
    unnamed x15, waiting for transfers between devices  231 us
    all_gather x4, blocking collectives, gather_layer(): lax.all_gather(ln_par, axis_name, axis=1, tiled=True)  135 us
    unnamed x2, blocking collectives  129 us
    all_gather x2, blocking collectives, gather_layer(): lax.all_gather(b_attn, axis_name, axis=1, tiled=True)  72.2 us
    convert_element_type x2, other arithmetic, layer_backward(): (probs_f32 * (d_probs - jnp.sum(d_probs * probs_f32, axis=-1, keepdims=Tr...  55.6 us
    dot_general x2, matrix products, layer_backward(): jnp.einsum('blf,bld->fd', act_bf, d_out, preferred_element_type=jnp.float32)  52 us
  transfers between devices with their start and end apart: 14, of which 5 were waited for; matrix products, arithmetic and copies ran while one was open for 25% of the time, Pallas kernels for 0%

commit v1 on v0

v1 whole, which is shorter than its diff:
```python
import math
import functools
import jax
import jax.numpy as jnp
from jax import lax
from jax.experimental import pallas as pl
from jax.experimental.pallas import tpu as pltpu
from jax.sharding import PartitionSpec as P

ZERO, ONE, TWO, THREE, FOUR = range(5)
EIGHT, SIXTEEN, WIDTH = 8, 16, 256

F32, BF16 = jnp.float32, jnp.bfloat16
SEQS, TOK, DIM, FFN, HEADS, HEAD, LANES = FOUR, 512, 512, 2048, EIGHT, 64, 128
HALF = HEAD // TWO
EPS = 1e-5
THETA = 10000.0
NEG_BIG = -1e30
B_ATTN, LN_PAR, B_UP, B_DOWN = ZERO, FOUR, EIGHT, 12


def nn(a, b):
    return lax.dot_general(a, b, (((ONE,), (ZERO,)), ((), ())), preferred_element_type=F32)


def nt(a, b):
    return lax.dot_general(a, b, (((ONE,), (ONE,)), ((), ())), preferred_element_type=F32)


def tn(a, b):
    return lax.dot_general(a, b, (((ZERO,), (ZERO,)), ((), ())), preferred_element_type=F32)


def lane_tiles(width=TOK, size=LANES):
    return [slice(i, i + size) for i in range(ZERO, width, size)]


def column(c_ref, lane, width=LANES):
    return jnp.broadcast_to(c_ref[:, lane:lane + ONE], (c_ref.shape[ZERO], width))


def total(value):
    return jnp.sum(value, axis=ZERO, keepdims=True)


def normed(x):
    centred = x - total(x) * (1.0 / DIM)
    rstd = lax.rsqrt(total(centred * centred) * (1.0 / DIM) + EPS)
    return centred * rstd, rstd


def norm_to(x_ref, c_ref, lane, h_ref):
    gain, shift = column(c_ref, lane), column(c_ref, lane + ONE)
    for cols in lane_tiles():
        h_ref[:, cols] = (normed(x_ref[:, cols].astype(F32))[ZERO] * gain + shift).astype(BF16)


def fold(value):
    parts = [value[:, cols] for cols in lane_tiles(value.shape[ONE])]
    return functools.reduce(jnp.add, parts)


def attn_fwd_kernel(first, len_ref, x_ref, w_ref, c_ref, cos_ref, sin_ref, *refs):
    if first:
        xt_ref, q_ref, k_ref, v_ref, p_ref, ctx_ref, h_ref, acc_ref = refs
        xt_ref[ZERO] = x_ref[ZERO].T
        xt_ref = xt_ref.at[ZERO]
    else:
        q_ref, k_ref, v_ref, p_ref, ctx_ref, h_ref, acc_ref = refs
        xt_ref = x_ref.at[ZERO]
    length = len_ref[pl.program_id(ZERO)]
    norm_to(xt_ref, c_ref, LN_PAR, h_ref)
    for m, out in enumerate((q_ref, k_ref, v_ref)):
        acc_ref[...] = nn(w_ref[m], h_ref[...])
        if m < TWO:
            scale = HEAD ** -0.5 if m == ZERO else 1.0
            for cols in lane_tiles():
                bias = column(c_ref, B_ATTN + m)
                for head in range(HEADS):
                    one, two = slice(HEAD * head, HEAD * head + HALF), slice(HEAD * head + HALF, HEAD * head + HEAD)
                    a = (acc_ref[one, cols] + bias[one]) * scale
                    b = (acc_ref[two, cols] + bias[two]) * scale
                    cos, sin = cos_ref[:, cols], sin_ref[:, cols]
                    out[ZERO, one, cols] = (a * cos - b * sin).astype(BF16)
                    out[ZERO, two, cols] = (b * cos + a * sin).astype(BF16)
        else:
            for cols in lane_tiles():
                out[ZERO, :, cols] = (acc_ref[:, cols] + column(c_ref, B_ATTN + m)).astype(BF16)

    key = lax.broadcasted_iota(jnp.int32, (SIXTEEN, TOK), ONE)
    row = lax.broadcasted_iota(jnp.int32, (SIXTEEN, TOK), ZERO)
    bias_rows = jnp.where((row == ZERO) & (key >= length), NEG_BIG, 0.0).astype(BF16)
    one_rows = jnp.where(row == ZERO, 1.0, 0.0).astype(BF16)

    @pl.loop(ZERO, HEADS)
    def _(head):
        rows = pl.ds(pl.multiple_of(head * HEAD, HEAD), HEAD)
        keys = jnp.concatenate([k_ref[ZERO, rows, :], bias_rows], axis=ZERO)
        for cols in lane_tiles(TOK, WIDTH):
            queries = jnp.concatenate([q_ref[ZERO, rows, cols], one_rows[:, cols]], axis=ZERO)
            scores = tn(keys, queries)
            weight = jnp.exp(scores - jnp.max(scores, axis=ZERO, keepdims=True))
            probs = (weight * (1.0 / total(weight))).astype(BF16)
            p_ref[ZERO, head, :, cols] = probs
            ctx_ref[ZERO, rows, cols] = nn(v_ref[ZERO, rows, :], probs)


def mlp_fwd_kernel(last, ctx_ref, x_ref, wo_ref, up_ref, *refs):
    if last:
        c_ref, mid_ref, act_ref, slope_ref, h_ref = refs
    else:
        down_ref, c_ref, mid_ref, act_ref, slope_ref, y_ref, h_ref = refs
    attn = nn(wo_ref[...], ctx_ref[ZERO].astype(BF16))
    for cols in lane_tiles():
        mid_ref[ZERO, :, cols] = (x_ref[ZERO, :, cols].astype(F32) + attn[:, cols] + column(c_ref, B_ATTN + THREE)).astype(BF16)
    norm_to(mid_ref.at[ZERO], c_ref, LN_PAR + TWO, h_ref)
    for part in range(FFN // DIM):
        rows = slice(DIM * part, DIM * part + DIM)
        pre = nn(up_ref[rows, :], h_ref[...])
        for cols in lane_tiles():
            z = pre[:, cols] + column(c_ref, B_UP + part)
            cdf = 0.5 * (1.0 + lax.erf(z * (1.0 / math.sqrt(2.0))))
            density = jnp.exp(-0.5 * z * z) * (1.0 / math.sqrt(2.0 * math.pi))
            act_ref[ZERO, rows, cols] = (z * cdf).astype(BF16)
            slope_ref[ZERO, rows, cols] = cdf + z * density
    if not last:
        out = nn(down_ref[...], act_ref[ZERO])
        for cols in lane_tiles():
            y_ref[ZERO, :, cols] = (mid_ref[ZERO, :, cols].astype(F32) + out[:, cols] + column(c_ref, B_DOWN)).astype(BF16)


def norm_back(dh, x, gain):
    xhat, rstd = normed(x)
    dxhat = dh * gain
    mean_one = total(dxhat) * (1.0 / DIM)
    mean_two = total(dxhat * xhat) * (1.0 / DIM)
    return rstd * (dxhat - mean_one - xhat * mean_two), xhat


def put_columns(out_ref, columns):
    lane = lax.broadcasted_iota(jnp.int32, (DIM, LANES), ONE)
    value = jnp.zeros((DIM, LANES), F32)
    for at, partial in columns:
        value = jnp.where(lane == at, jnp.sum(partial, axis=ONE, keepdims=True), value)
    out_ref[...] = value


def mlp_bwd_kernel(last, dy_ref, slope_ref, act_ref, mid_ref, ctx_ref, wo_ref, up_ref, down_ref, c_ref,
                   dmid_ref, dctx_ref, gwo_ref, gup_ref, gdown_ref, gc_ref, dyt_ref, dpre_ref, h_ref, dh_ref, sums_ref):
    seq = pl.program_id(ZERO)

    @pl.when(seq == ZERO)
    def _():
        for ref in (gwo_ref, gup_ref, gdown_ref, sums_ref):
            ref[...] = jnp.zeros_like(ref)

    if last:
        dyt_ref[...] = dy_ref[ZERO].T
    else:
        dyt_ref[...] = dy_ref[ZERO]
    norm_to(mid_ref.at[ZERO], c_ref, LN_PAR + TWO, h_ref)
    for part in range(FFN // DIM):
        rows = slice(DIM * part, DIM * part + DIM)
        dact = nn(down_ref[rows, :], dyt_ref[...])
        for cols in lane_tiles():
            dpre = dact[:, cols] * slope_ref[ZERO, rows, cols]
            sums_ref[part] += dpre
            dpre_ref[rows, cols] = dpre.astype(BF16)
        gdown_ref[rows, :] += nt(act_ref[ZERO, rows, :], dyt_ref[...])
        gup_ref[:, rows] += nt(h_ref[...], dpre_ref[rows, :])
    dh_ref[...] = nn(up_ref[...], dpre_ref[...])
    gain = column(c_ref, LN_PAR + TWO)
    for cols in lane_tiles():
        dh, dy = dh_ref[:, cols], dyt_ref[:, cols].astype(F32)
        dx, xhat = norm_back(dh, mid_ref[ZERO, :, cols].astype(F32), gain)
        dmid = (dy + dx).astype(BF16)
        dmid_ref[ZERO, :, cols] = dmid
        sums_ref[FOUR] += dh * xhat
        sums_ref[5] += dh
        sums_ref[6] += dy
        sums_ref[7] += dmid.astype(F32)
    gwo_ref[...] += nt(ctx_ref[ZERO].astype(BF16), dmid_ref[ZERO])
    dctx_ref[ZERO] = nn(wo_ref[...], dmid_ref[ZERO]).astype(BF16)

    @pl.when(seq == SEQS - ONE)
    def _():
        put_columns(gc_ref, [(B_UP + i, sums_ref[i]) for i in range(FOUR)] + [
            (LN_PAR + TWO, sums_ref[FOUR]), (LN_PAR + THREE, sums_ref[5]), (B_DOWN, sums_ref[6]), (B_ATTN + THREE, sums_ref[7])])


def attn_bwd_kernel(first, dctx_ref, ctx_ref, p_ref, q_ref, k_ref, v_ref, x_ref, dmid_ref, w_ref, c_ref, cos_ref, sin_ref,
                    dx_ref, gw_ref, gc_ref, dq_ref, dk_ref, dproj_ref, h_ref, dh_ref, sums_ref):
    seq = pl.program_id(ZERO)

    @pl.when(seq == ZERO)
    def _():
        gw_ref[...] = jnp.zeros_like(gw_ref)
        sums_ref[...] = jnp.zeros_like(sums_ref)

    @pl.loop(ZERO, HEADS)
    def _(head):
        rows = pl.ds(pl.multiple_of(head * HEAD, HEAD), HEAD)
        dk = jnp.zeros((HEAD, TOK), F32)
        dv = jnp.zeros((HEAD, TOK), F32)
        for cols in lane_tiles(TOK, WIDTH):
            dctx = dctx_ref[ZERO, rows, cols]
            delta = total(dctx.astype(F32) * ctx_ref[ZERO, rows, cols])
            dprobs = tn(v_ref[ZERO, rows, :], dctx)
            probs = p_ref[ZERO, head, :, cols]
            dscores = (probs.astype(F32) * (dprobs - delta)).astype(BF16)
            dv = dv + nt(dctx, probs)
            dk = dk + nt(q_ref[ZERO, rows, cols], dscores)
            dq_ref[rows, cols] = nn(k_ref[ZERO, rows, :], dscores)
        dk_ref[rows, :] = dk
        sums_ref[TWO, rows, :] += fold(dv)
        dproj_ref[TWO, rows, :] = dv.astype(BF16)

    for m, (ref, scale) in enumerate(((dq_ref, HEAD ** -0.5), (dk_ref, 1.0))):
        for cols in lane_tiles():
            for head in range(HEADS):
                one, two = slice(HEAD * head, HEAD * head + HALF), slice(HEAD * head + HALF, HEAD * head + HEAD)
                a, b = ref[one, cols] * scale, ref[two, cols] * scale
                cos, sin = cos_ref[:, cols], sin_ref[:, cols]
                for rows, value in ((one, a * cos + b * sin), (two, b * cos - a * sin)):
                    dproj_ref[m, rows, cols] = value.astype(BF16)
                    sums_ref[m, rows, :] += value
    norm_to(x_ref.at[ZERO], c_ref, LN_PAR, h_ref)
    for m in range(THREE):
        gw_ref[m] += nt(h_ref[...], dproj_ref[m])
    dh_ref[...] = functools.reduce(jnp.add, [nn(w_ref[m], dproj_ref[m]) for m in range(THREE)])
    gain = column(c_ref, LN_PAR)
    for cols in lane_tiles():
        dh = dh_ref[:, cols]
        dx, xhat = norm_back(dh, x_ref[ZERO, :, cols].astype(F32), gain)
        dx = (dmid_ref[ZERO, :, cols].astype(F32) + dx).astype(BF16)
        if first:
            dx_ref[ZERO, cols, :] = dx.T
        else:
            dx_ref[ZERO, :, cols] = dx
        sums_ref[THREE] += dh * xhat
        sums_ref[FOUR] += dh

    @pl.when(seq == SEQS - ONE)
    def _():
        put_columns(gc_ref, [(B_ATTN + i, sums_ref[i]) for i in range(THREE)] + [(LN_PAR, sums_ref[THREE]), (LN_PAR + ONE, sums_ref[FOUR])])


def seq_spec(shape):
    return pl.BlockSpec((ONE, *shape), lambda s: (s,) + (ZERO,) * len(shape))


def once(shape):
    return pl.BlockSpec(shape, lambda s: (ZERO,) * len(shape), pipeline_mode=pl.Buffered(ONE))


def act_shape(rows, dtype):
    return jax.ShapeDtypeStruct((SEQS, rows, TOK), dtype)


PARAMS = pltpu.CompilerParams(vmem_limit_bytes=60 << 20, dimension_semantics=("arbitrary",))
SQUARE, TALL, WIDE, COLS = (DIM, TOK), (FFN, TOK), (DIM, FFN), (DIM, LANES)


def attn_fwd(first, lengths, x, w, c, tables):
    smem = pl.BlockSpec(memory_space=pltpu.SMEM)
    outs = [act_shape(DIM, BF16)] * (FOUR if first else THREE)
    return pl.pallas_call(
        functools.partial(attn_fwd_kernel, first), grid=(SEQS,),
        out_shape=outs + [jax.ShapeDtypeStruct((SEQS, HEADS, TOK, TOK), BF16), act_shape(DIM, F32)],
        in_specs=[smem, seq_spec(SQUARE), once((THREE, DIM, DIM)), once(COLS), once((HALF, TOK)), once((HALF, TOK))],
        out_specs=[seq_spec(SQUARE)] * len(outs) + [seq_spec((HEADS, TOK, TOK)), seq_spec(SQUARE)],
        scratch_shapes=[pltpu.VMEM(SQUARE, BF16), pltpu.VMEM(SQUARE, F32)], compiler_params=PARAMS,
        name="attn_fwd")(lengths, x, w, c, *tables)


def mlp_fwd(last, ctx, x, wo, up, down, c):
    downs = [] if last else [down]
    return pl.pallas_call(
        functools.partial(mlp_fwd_kernel, last), grid=(SEQS,),
        out_shape=[act_shape(DIM, BF16), act_shape(FFN, BF16), act_shape(FFN, F32)] + [act_shape(DIM, BF16)] * len(downs),
        in_specs=[seq_spec(SQUARE)] * TWO + [once((DIM, DIM)), once((FFN, DIM))] + [once(WIDE)] * len(downs) + [once(COLS)],
        out_specs=[seq_spec(SQUARE), seq_spec(TALL), seq_spec(TALL)] + [seq_spec(SQUARE)] * len(downs),
        scratch_shapes=[pltpu.VMEM(SQUARE, BF16)], compiler_params=PARAMS, name="mlp_fwd")(ctx, x, wo, up, *downs, c)


def mlp_bwd(last, dy, slope, act, mid, ctx, wo, up, down, c):
    return pl.pallas_call(
        functools.partial(mlp_bwd_kernel, last), grid=(SEQS,),
        out_shape=[act_shape(DIM, BF16)] * TWO + [jax.ShapeDtypeStruct(s, F32) for s in ((DIM, DIM), WIDE, (FFN, DIM), COLS)],
        in_specs=[seq_spec(SQUARE), seq_spec(TALL), seq_spec(TALL), seq_spec(SQUARE), seq_spec(SQUARE),
                  once((DIM, DIM)), once(WIDE), once((FFN, DIM)), once(COLS)],
        out_specs=[seq_spec(SQUARE)] * TWO + [once((DIM, DIM)), once(WIDE), once((FFN, DIM)), once(COLS)],
        scratch_shapes=[pltpu.VMEM(SQUARE, BF16), pltpu.VMEM(TALL, BF16), pltpu.VMEM(SQUARE, BF16), pltpu.VMEM(SQUARE, F32),
                        pltpu.VMEM((EIGHT, DIM, LANES), F32)],
        compiler_params=PARAMS, name="mlp_bwd")(dy, slope, act, mid, ctx, wo, up, down, c)


def attn_bwd(first, dctx, ctx, probs, q, k, v, x, dmid, w, c, tables):
    return pl.pallas_call(
        functools.partial(attn_bwd_kernel, first), grid=(SEQS,),
        out_shape=[act_shape(DIM, BF16), jax.ShapeDtypeStruct((THREE, DIM, DIM), F32), jax.ShapeDtypeStruct(COLS, F32)],
        in_specs=[seq_spec(SQUARE)] * TWO + [seq_spec((HEADS, TOK, TOK))] + [seq_spec(SQUARE)] * 5 + [
            once((THREE, DIM, DIM)), once(COLS), once((HALF, TOK)), once((HALF, TOK))],
        out_specs=[seq_spec(SQUARE), once((THREE, DIM, DIM)), once(COLS)],
        scratch_shapes=[pltpu.VMEM(SQUARE, F32)] * TWO + [pltpu.VMEM((THREE, *SQUARE), BF16), pltpu.VMEM(SQUARE, BF16),
                        pltpu.VMEM(SQUARE, F32), pltpu.VMEM((5, DIM, LANES), F32)],
        compiler_params=PARAMS, name="attn_bwd")(dctx, ctx, probs, q, k, v, x, dmid, w, c, *tables)


def rotary_tables():
    inv_freq = 1.0 / (THETA ** (jnp.arange(HALF, dtype=F32) * (2.0 / HEAD)))
    angles = inv_freq[:, None] * jnp.arange(TOK, dtype=F32)[None, :]
    return jnp.cos(angles), jnp.sin(angles)


MESH = pl.DeviceIdType.MESH
AXIS = "fsdp"
ORDERS = ((TWO, ONE, ZERO), (ONE, ZERO, TWO), (ZERO, TWO, ONE))


class Place:
    def __init__(self):
        me = lax.axis_index(AXIS)
        self.me = me
        self.core = lax.rem(me, TWO)
        self.pos = (me // 32, lax.rem(me // EIGHT, FOUR), lax.rem(me // TWO, FOUR))
        self.partner = me + ONE - TWO * self.core

    def coord(self, dim, delta):
        return lax.rem(self.pos[dim] + (delta + FOUR), FOUR)

    def device(self, dim, delta):
        pos = list(self.pos)
        pos[dim] = self.coord(dim, delta)
        return pos[ZERO] * 32 + pos[ONE] * EIGHT + pos[TWO] * TWO + self.core

    def greet(self, reach=(ONE, -ONE)):
        self.greeted = THREE * len(reach) + ONE
        barrier = pltpu.get_barrier_semaphore()
        for dim in range(THREE):
            for delta in reach:
                pl.semaphore_signal(barrier, inc=ONE, device_id=(self.device(dim, delta),), device_id_type=MESH)
        pl.semaphore_signal(barrier, inc=ONE, device_id=(self.partner,), device_id_type=MESH)

    def met(self):
        pl.semaphore_wait(pltpu.get_barrier_semaphore(), self.greeted)


def remote(src, dst, send_sem, recv_sem, device):
    return pltpu.make_async_remote_copy(src_ref=src, dst_ref=dst, send_sem=send_sem, recv_sem=recv_sem,
                                        device_id=(device,), device_id_type=MESH)


class Gather:
    def __init__(self, place, buf, order, send, recv):
        self.place, self.buf, self.order, self.send, self.recv = place, buf, order, send, recv
        self.units = buf.shape[FOUR]

    def where(self, stage, at, half=None):
        dim = self.order[stage]
        index = list(self.place.pos)
        index[dim] = at
        for done in self.order[:stage]:
            index[done] = slice(ZERO, FOUR)
        unit = slice(ZERO, self.units)
        if half is not None:
            if stage > ZERO:
                index[self.order[ZERO]] = pl.ds(TWO * half, TWO)
            else:
                cut = (self.units + ONE) // TWO
                unit = slice(ZERO, cut) if half == ZERO else slice(cut, self.units)
        index = [pl.ds(i, ONE) if not isinstance(i, (slice, pl.Slice)) else i for i in index]
        return self.buf.at[index[ZERO], index[ONE], index[TWO], pl.ds(self.place.core, ONE), unit]

    def copies(self, stage, step, way):
        place, dim = self.place, self.order[stage]
        delta = ONE if way == ZERO else -ONE
        key = (stage * TWO + step) * TWO + way
        if step == ZERO:
            mine = self.where(stage, place.pos[dim])
            came = self.where(stage, place.coord(dim, -delta))
        else:
            if stage == ZERO and self.units == ONE and way == ONE:
                return None, None
            mine = self.where(stage, place.coord(dim, -delta), way)
            came = self.where(stage, place.coord(dim, -TWO * delta), way)
        def build(ref):
            return remote(ref, ref, self.send.at[key], self.recv.at[key], place.device(dim, delta))

        return lambda: build(mine), lambda: build(came)

    def step_a(self, stage):
        for way in (ZERO, ONE):
            self.copies(stage, ZERO, way)[ZERO]().start()

    def step_b(self, stage):
        for way in (ZERO, ONE):
            self.copies(stage, ZERO, way)[ONE]().wait_recv()
            out = self.copies(stage, ONE, way)[ZERO]
            if out is not None:
                out().start()

    def step_c(self, stage):
        for way in (ZERO, ONE):
            inc = self.copies(stage, ONE, way)[ONE]
            if inc is not None:
                inc().wait_recv()

    def share(self):
        half = self.buf.at[:, :, :, pl.ds(self.place.core, ONE)]
        return remote(half, half, self.send.at[12], self.recv.at[12], self.place.partner)

    def shared(self):
        half = self.buf.at[:, :, :, pl.ds(ONE - self.place.core, ONE)]
        remote(half, half, self.send.at[12], self.recv.at[12], self.place.partner).wait_recv()

    def drain(self):
        for stage in range(THREE):
            for step in range(TWO):
                for way in (ZERO, ONE):
                    out = self.copies(stage, step, way)[ZERO]
                    if out is not None:
                        out().wait_send()
        self.share().wait_send()


def gather_all(gathers):
    for stage in range(THREE):
        for g in gathers:
            g.step_a(stage)
        for g in gathers:
            g.step_b(stage)
        for g in gathers:
            g.step_c(stage)
    for g in gathers:
        g.share().start()
    for g in gathers:
        g.shared()
    for g in gathers:
        g.drain()


class Scatter:
    def __init__(self, place, grads, acc, got_a, got_b, order, send, recv):
        self.place, self.grads, self.acc, self.order = place, grads, acc, order
        self.got_a, self.got_b, self.send, self.recv = got_a, got_b, send, recv
        self.units = acc.shape[ZERO]

    def columns(self, core):
        return pl.ds(pl.multiple_of(core * WIDTH, WIDTH), WIDTH)

    def swap(self):
        place = self.place
        for u in range(self.units):
            remote(self.grads(u).at[:, :, :, :, self.columns(ONE - place.core)], self.acc.at[u],
                   self.send.at[20 + u], self.recv.at[20 + u], place.partner).start()

    def swapped(self):
        place = self.place
        for u in range(self.units):
            copy = remote(self.grads(u).at[:, :, :, :, self.columns(ONE - place.core)], self.acc.at[u],
                          self.send.at[20 + u], self.recv.at[20 + u], place.partner)
            copy.wait_recv()
            grad, acc = self.grads(u), self.acc

            @pl.loop(ZERO, SIXTEEN)
            def _(i):
                z, y = i // FOUR, lax.rem(i, FOUR)
                acc[u, z, y] = acc[u, z, y] + grad[z, y, :, :, self.columns(place.core)]

    def index(self, stage, at):
        index = [slice(ZERO, FOUR)] * THREE
        for done in self.order[:stage]:
            index[done] = pl.ds(self.place.pos[done], ONE)
        index[self.order[stage]] = pl.ds(at, ONE)
        return index

    def part(self, stage, at, half=None):
        columns = slice(ZERO, WIDTH) if half is None else slice(128 * half, 128 * half + 128)
        return self.acc.at[(slice(ZERO, self.units), *self.index(stage, at), slice(ZERO, EIGHT), columns)]

    def copy(self, stage, step, way):
        place, dim = self.place, self.order[stage]
        delta = ONE if way == ZERO else -ONE
        key = (stage * TWO + step) * TWO + way
        if step == ZERO:
            src, ref, half = self.part(stage, place.coord(dim, TWO), way), self.got_a, way
        else:
            src, ref, half = self.part(stage, place.coord(dim, delta)), self.got_b, None
        return src, ref, half, key, place.device(dim, delta)

    def start(self, stage, step, way):
        src, ref, half, key, device = self.copy(stage, step, way)
        remote(src, self.cast(ref, stage, way, half, src), self.send.at[key], self.recv.at[key], device).start()

    def wait(self, stage, step, way):
        src, ref, half, key, device = self.copy(stage, step, way)
        remote(src, self.cast(ref, stage, way, half, src), self.send.at[key], self.recv.at[key], device).wait_recv()

    def cast(self, ref, stage, way, half, src):
        columns = slice(ZERO, WIDTH) if half is None else slice(128 * half, 128 * half + 128)
        return ref[stage].at[(ZERO if half is not None else way, slice(ZERO, self.units), *([slice(None)] * THREE), slice(ZERO, EIGHT), columns)]

    def add(self, stage, at, refs, half):
        units = self.units
        shape = self.got_b[stage].shape[TWO:5]
        total = units * shape[ZERO] * shape[ONE] * shape[TWO]
        columns = slice(ZERO, WIDTH) if half is None else slice(128 * half, 128 * half + 128)
        base = [ZERO, ZERO, ZERO]
        for done in self.order[:stage]:
            base[done] = self.place.pos[done]
        base[self.order[stage]] = at
        acc = self.acc
        bunch = FOUR if total % FOUR == ZERO else ONE

        @pl.loop(ZERO, total // bunch)
        def _(k):
            for j in range(bunch):
                i = k * bunch + j
                u = i // (shape[ZERO] * shape[ONE] * shape[TWO])
                a = lax.rem(i // (shape[ONE] * shape[TWO]), shape[ZERO])
                b = lax.rem(i // shape[TWO], shape[ONE])
                c = lax.rem(i, shape[TWO])
                here = (u, base[ZERO] + a, base[ONE] + b, base[TWO] + c, slice(ZERO, EIGHT), columns)
                value = acc[here]
                for ref, way in refs:
                    value = value + ref[stage][ZERO if half is not None else way, u, a, b, c, :, columns]
                acc[here] = value

    def step_a(self, stage):
        for way in (ZERO, ONE):
            self.start(stage, ZERO, way)

    def step_b(self, stage):
        dim = self.order[stage]
        for way in (ZERO, ONE):
            delta = ONE if way == ZERO else -ONE
            self.wait(stage, ZERO, way)
            self.add(stage, self.place.coord(dim, delta), [(self.got_a, way)], way)
            self.start(stage, ONE, way)

    def step_c(self, stage):
        dim = self.order[stage]
        for way in (ZERO, ONE):
            self.wait(stage, ONE, way)
        self.add(stage, self.place.pos[dim], [(self.got_b, ZERO), (self.got_b, ONE)], None)

    def last(self, own, other):
        place = self.place
        z, y, x = place.pos
        src = self.acc.at[:, z, y, x]
        return remote(src, other, self.send.at[12], self.recv.at[12], place.partner)

    def drain(self, other):
        for stage in range(THREE):
            for step in range(TWO):
                for way in (ZERO, ONE):
                    src, ref, half, key, device = self.copy(stage, step, way)
                    remote(src, self.cast(ref, stage, way, half, src), self.send.at[key], self.recv.at[key], device).wait_send()
        for u in range(self.units):
            remote(self.grads(u).at[:, :, :, :, self.columns(ONE - self.place.core)], self.acc.at[u],
                   self.send.at[20 + u], self.recv.at[20 + u], self.place.partner).wait_send()
        self.last(None, other).wait_send()

    def result(self, unit, other):
        z, y, x = self.place.pos
        own, came = self.acc[unit, z, y, x], other[unit]
        first = self.place.core == ZERO
        return jnp.concatenate([jnp.where(first, own, came), jnp.where(first, came, own)], axis=ONE)


def landing_shapes(order, units, ways):
    shapes = []
    for stage in range(THREE):
        size = [FOUR, FOUR, FOUR]
        for done in order[:stage + ONE]:
            size[done] = ONE
        shapes.append((ways, units, *size, EIGHT, WIDTH))
    return shapes


class Small:
    def __init__(self, place, value, slots, send, recv):
        self.place, self.value, self.slots, self.send, self.recv = place, value, slots, send, recv

    def copies(self, stage):
        if stage == THREE:
            return [remote(self.value, self.slots.at[9], self.send.at[9], self.recv.at[9], self.place.partner)]
        return [remote(self.value, self.slots.at[stage * THREE + k], self.send.at[stage * THREE + k], self.recv.at[stage * THREE + k],
                       self.place.device(stage, delta)) for k, delta in enumerate((ONE, -ONE, TWO))]

    def start(self, stage):
        for copy in self.copies(stage):
            copy.start()

    def finish(self, stage):
        copies = self.copies(stage)
        for copy in copies:
            copy.wait()
        value = self.value[...]
        for k in range(len(copies)):
            value = value + self.slots[stage * THREE + k]
        self.value[...] = value


COLOURS = ((ZERO, THREE, FOUR, 5), (ONE, 6, 7, EIGHT), (TWO, 9, 10, 11))
KEYS = 28


def each_unit():
    for colour in range(THREE):
        for layer in range(TWO):
            for slot, unit in enumerate(COLOURS[colour]):
                yield colour, layer, layer * FOUR + slot, unit


def gather_kernel(packed, small, attn_out, up_out, down_out, attn_t, up_t, down_t, small_out, buf0, buf1, buf2, buf3, send, recv, local):
    place = Place()
    place.greet()
    z, y, x = place.pos
    bufs = (buf0, buf1, buf2)
    copies = [pltpu.make_async_copy(packed.at[k], bufs[k].at[z, y, x, place.core], local.at[k]) for k in range(THREE)]
    copies.append(pltpu.make_async_copy(small, buf3.at[z, y, x, place.core], local.at[THREE]))
    for copy in copies:
        copy.start()
    for copy in copies:
        copy.wait()
    place.met()
    gathers = [Gather(place, bufs[k], ORDERS[k], send.at[k], recv.at[k]) for k in range(THREE)]
    gathers.append(Gather(place, buf3, ORDERS[ZERO], send.at[THREE], recv.at[THREE]))
    gather_all(gathers)
    small_out[...] = buf3[...]

    for colour, layer, u, unit in each_unit():
        buf = bufs[colour]
        if unit < EIGHT:
            @pl.loop(ZERO, 32)
            def _(g):
                tiles = [buf[g // EIGHT, lax.rem(g // TWO, FOUR), lax.rem(g, TWO) * TWO + k // TWO, k % TWO, u].astype(F32) for k in range(FOUR)]
                rows = pl.ds(pl.multiple_of(g * SIXTEEN, SIXTEEN), SIXTEEN)
                for j, cols in enumerate(lane_tiles()):
                    block = jnp.concatenate([t[FOUR * j:FOUR * j + FOUR] for t in tiles], axis=ZERO).astype(BF16)
                    if unit < FOUR:
                        attn_out[layer, unit, rows, cols] = block
                    else:
                        up_out[layer, rows, DIM * (unit - FOUR) + cols.start:DIM * (unit - FOUR) + cols.stop] = block
        else:
            @pl.loop(ZERO, LANES)
            def _(d):
                rows = pl.ds(pl.multiple_of(d * SIXTEEN, SIXTEEN), SIXTEEN)
                down_out[layer, rows, lane_tiles()[unit - EIGHT]] = buf[d // 32, lax.rem(d // EIGHT, FOUR), lax.rem(d // TWO, FOUR), lax.rem(d, TWO), u]
    for layer in range(TWO):
        for k in range(FOUR):
            attn_t[layer, k] = attn_out[layer, k].T
            part = slice(DIM * k, DIM * k + DIM)
            up_t[layer, part, :] = up_out[layer, :, part].T
            down_t[layer, :, part] = down_out[layer, part, :].T


VMEM = pl.BlockSpec(memory_space=pltpu.VMEM)
HBM = pl.BlockSpec(memory_space=pl.ANY)
DMA = pltpu.SemaphoreType.DMA


def gather_params(packed, small):
    shapes = ((TWO, FOUR, DIM, DIM), (TWO, *WIDE), (TWO, FFN, DIM))
    both = shapes + (shapes[ZERO], shapes[TWO], shapes[ONE])
    tiny = (FOUR, FOUR, FOUR, TWO, ONE, ONE, LANES)
    return pl.pallas_call(
        gather_kernel,
        out_shape=[jax.ShapeDtypeStruct(s, BF16) for s in both] + [jax.ShapeDtypeStruct(tiny, F32)],
        in_specs=[HBM] * TWO,
        out_specs=[VMEM] * 7,
        scratch_shapes=[pltpu.VMEM((FOUR, FOUR, FOUR, TWO, EIGHT, SIXTEEN, LANES), BF16)] * THREE + [pltpu.VMEM(tiny, F32), DMA((FOUR, 13)), DMA((FOUR, 13)), DMA((FOUR,))],
        compiler_params=pltpu.CompilerParams(collective_id=ZERO, has_side_effects=True, vmem_limit_bytes=60 << 20),
        name="gather_params")(packed, small)


def scatter_kernel(*refs):
    place = Place()
    place.greet((ONE, -ONE, TWO))
    weights, refs = (refs[:FOUR], refs[FOUR:EIGHT]), refs[EIGHT:]
    small, attn_out, up_out, down_out, small_out = refs[:5]
    grads, accs, others, (sm, slots), refs = refs[5:EIGHT], refs[EIGHT:11], refs[11:14], refs[14:SIXTEEN], refs[SIXTEEN:]
    got_a = [refs[THREE * k:THREE * k + THREE] for k in range(THREE)]
    got_b = [refs[9 + THREE * k:9 + THREE * k + THREE] for k in range(THREE)]
    send, recv, ssend, srecv, local = refs[18:]
    copies = []
    for colour, layer, u, unit in each_unit():
        qkv, out, up, down = weights[layer]
        if unit < THREE:
            src = qkv.at[unit]
        elif unit == THREE:
            src = out
        elif unit < EIGHT:
            src = up.at[:, :, :, :, pl.ds(DIM * (unit - FOUR), DIM)]
        else:
            src = down.at[:, :, :, unit - EIGHT]
        copies.append(pltpu.make_async_copy(src, grads[colour].at[u], local.at[colour]))
    copies.append(pltpu.make_async_copy(small, sm, local.at[THREE]))
    for copy in copies:
        copy.start()
    for copy in copies:
        copy.wait()
    place.met()
    scatters = [Scatter(place, (lambda u, k=k: grads[k].at[u]), accs[k], got_a[k], got_b[k], ORDERS[k], send.at[k], recv.at[k])
                for k in range(THREE)]
    tiny = Small(place, sm, slots, ssend, srecv)
    for s in scatters:
        s.swap()
    tiny.start(ZERO)
    for s in scatters:
        s.swapped()
        s.step_a(ZERO)
    for stage in range(THREE):
        if stage:
            for s in scatters:
                s.step_a(stage)
        for s in scatters:
            s.step_b(stage)
        tiny.finish(stage)
        tiny.start(stage + ONE)
        for s in scatters:
            s.step_c(stage)
    for s, other in zip(scatters, others):
        s.last(None, other).start()
    tiny.finish(THREE)
    for s, other in zip(scatters, others):
        s.last(None, other).wait_recv()
    small_out[...] = sm[...]
    first = place.core == ZERO
    for colour, layer, u, unit in each_unit():
        full = scatters[colour].result(u, others[colour])
        if unit < EIGHT:
            mine = jnp.where(first, full[:FOUR], full[FOUR:])
            if unit < FOUR:
                attn_out[layer, unit] = mine
            else:
                up_out[layer, :, DIM * (unit - FOUR):DIM * (unit - THREE)] = mine
        else:
            at = EIGHT * (unit % TWO)

            @pl.when(place.core == (unit - EIGHT) // TWO)
            def _():
                down_out[layer, at:at + EIGHT] = full
    for s, other in zip(scatters, others):
        s.drain(other)


def scatter_grads(weights, small):
    acc, tiny = (EIGHT, FOUR, FOUR, FOUR, EIGHT, WIDTH), (32, DIM)
    scratch = [pltpu.VMEM((EIGHT, FOUR, FOUR, FOUR, EIGHT, DIM), F32)] * THREE + [pltpu.VMEM(acc, F32)] * THREE + [pltpu.VMEM((EIGHT, EIGHT, WIDTH), F32)] * THREE
    scratch += [pltpu.VMEM(tiny, F32), pltpu.VMEM((10, *tiny), F32)]
    for ways in (ONE, TWO):
        for order in ORDERS:
            scratch += [pltpu.VMEM(s, F32) for s in landing_shapes(order, EIGHT, ways)]
    scratch += [DMA((THREE, KEYS)), DMA((THREE, KEYS)), DMA((10,)), DMA((10,)), DMA((FOUR,))]
    grid = (FOUR, FOUR, FOUR)
    flat = []
    for qkv, out, up, down in weights:
        flat += [qkv.reshape(THREE, *grid, EIGHT, DIM), out.reshape(*grid, EIGHT, DIM), up.reshape(*grid, EIGHT, FFN), down.reshape(*grid, FOUR, EIGHT, DIM)]
    return pl.pallas_call(
        scatter_kernel,
        out_shape=[jax.ShapeDtypeStruct(s, F32) for s in ((TWO, FOUR, FOUR, DIM), (TWO, FOUR, FFN), (TWO, SIXTEEN, DIM), tiny)],
        in_specs=[HBM] * 9,
        out_specs=[VMEM] * FOUR,
        scratch_shapes=scratch,
        compiler_params=pltpu.CompilerParams(collective_id=ONE, has_side_effects=True, vmem_limit_bytes=63 << 20),
        name="scatter_grads")(*flat, small)


def pack_shards(w_attn, w_up, w_down):
    attn = w_attn.reshape(TWO, FOUR, FOUR, FOUR, LANES).transpose(ZERO, ONE, THREE, TWO, FOUR).reshape(TWO, FOUR, SIXTEEN, LANES)
    up = w_up.reshape(TWO, FOUR, FOUR, FOUR, LANES).transpose(ZERO, TWO, THREE, ONE, FOUR).reshape(TWO, FOUR, SIXTEEN, LANES)
    down = w_down.reshape(TWO, SIXTEEN, FOUR, LANES).transpose(ZERO, TWO, ONE, THREE)
    units = jnp.concatenate([attn, up, down], axis=ONE)
    return jnp.stack([jnp.concatenate([units[layer, jnp.array(c)] for layer in range(TWO)], axis=ZERO) for c in COLOURS])


def pack_small(b_attn, ln_par, b_up, b_down):
    row = jnp.concatenate([b_attn.reshape(TWO, SIXTEEN), ln_par.reshape(TWO, SIXTEEN), b_up, b_down, jnp.zeros((TWO, 12), b_up.dtype)], axis=ONE)
    return row.reshape(ONE, ONE, LANES).astype(F32)


def small_columns(small):
    small = small.reshape(LANES, TWO, 64)
    parts = small[:, :, :32].reshape(LANES, TWO, EIGHT, FOUR).transpose(ONE, ZERO, THREE, TWO).reshape(TWO, DIM, EIGHT)
    ups = small[:, :, 32:48].transpose(ONE, ZERO, TWO).reshape(TWO, FOUR, DIM).transpose(ZERO, TWO, ONE)
    down = small[:, :, 48:52].transpose(ONE, ZERO, TWO).reshape(TWO, DIM, ONE)
    return jnp.pad(jnp.concatenate([parts, ups, down], axis=TWO), ((ZERO, ZERO), (ZERO, ZERO), (ZERO, LANES - 13)))


def solution(mesh):
    batch_spec = P(AXIS)
    weight_specs = (P(None, None, AXIS, None), P(None, None, AXIS), P(None, None, AXIS),
                    P(None, AXIS, None), P(None, AXIS), P(None, AXIS, None), P(None, AXIS))

    def device_step(x, lengths, d_y, w_attn, b_attn, ln_par, w_up, b_up, w_down, b_down):
        tables = rotary_tables()
        attn, up, down, attn_t, up_t, down_t, small = gather_params(pack_shards(w_attn, w_up, w_down), pack_small(b_attn, ln_par, b_up, b_down))
        columns = small_columns(small)
        saved = []
        for l in range(TWO):
            first, last = l == ZERO, l == ONE
            c = columns[l]
            outs = attn_fwd(first, lengths, x, attn_t[l, :THREE], c, tables)
            if first:
                x, *outs = outs
            q, k, v, probs, ctx = outs
            mid, act, slope, *rest = mlp_fwd(last, ctx, x, attn_t[l, THREE], up_t[l], down_t[l], c)
            saved.append((x, q, k, v, probs, ctx, mid, act, slope))
            if rest:
                x = rest[ZERO]
        grad, weights, rows = d_y, [None] * TWO, [None] * TWO
        for l in (ONE, ZERO):
            x, q, k, v, probs, ctx, mid, act, slope = saved[l]
            c = columns[l]
            dmid, dctx, gwo, gup, gdown, gc_mlp = mlp_bwd(l == ONE, grad, slope, act, mid, ctx, attn[l, THREE], up[l], down[l], c)
            grad, gw, gc_attn = attn_bwd(l == ZERO, dctx, ctx, probs, q, k, v, x, dmid, attn[l, :THREE], c, tables)
            weights[l] = (gw, gwo, gup, gdown)
            rows[l] = (gc_mlp + gc_attn)[:, :SIXTEEN].T
        attn, up, down, small = scatter_grads(weights, jnp.concatenate(rows))
        me = lax.axis_index(AXIS)
        small = small.reshape(TWO, SIXTEEN, DIM)
        mine = lax.dynamic_slice(small, (ZERO, ZERO, FOUR * me), (TWO, SIXTEEN, FOUR))
        b_up_grad = lax.dynamic_slice(small[:, B_UP:B_DOWN].reshape(TWO, FFN), (ZERO, SIXTEEN * me), (TWO, SIXTEEN))
        return grad, attn, mine[:, :FOUR], mine[:, FOUR:EIGHT], up, b_up_grad, down, mine[:, 12]

    return jax.shard_map(device_step, mesh=mesh,
                         in_specs=(batch_spec, batch_spec, batch_spec) + weight_specs,
                         out_specs=(batch_spec,) + weight_specs,
                         check_vma=False)
```

time: 2440 us -> 553 us (0.23)
  waiting for transfers between devices: 1330 us -> 0 us
  Pallas kernels: 0 us -> 496 us
  matrix products: 390 us -> 0 us
  blocking collectives: 336 us -> 0 us
  other arithmetic: 237 us -> 5.1 us
  local copies, waits for them, and re-layouts: 122 us -> 42.7 us
    reduce_scatter x2 -> x0, waiting for transfers between devices: 1060 us -> none  [scatter_grads(): reduce_rows(gw_down, scatter_dimension=0)]
    pallas_call x0 -> x10, Pallas kernels: none -> 496 us  [the longest x1 96.8 us: scatter_grads(): pl.pallas_call(scatter_kernel, out_shape=[jax.ShapeDtypeStruct(s, F32) fo...]
    dot_general x33 -> x0, matrix products: 351 us -> none  [the longest x2 52 us: layer_backward(): jnp.einsum('blf,bld->fd', act_bf, d_out, preferred_element_type=jnp.float32)]
    unnamed x15 -> x0, waiting for transfers between devices: 231 us -> none
    all_gather x6 -> x0, blocking collectives: 207 us -> none  [the longest x4 135 us: gather_layer(): lax.all_gather(ln_par, axis_name, axis=1, tiled=True)]
    convert_element_type x20 -> x0, other arithmetic: 156 us -> none  [the longest x2 55.6 us: layer_backward(): (probs_f32 * (d_probs - jnp.sum(d_probs * probs_f32, axis=-1, keepdims=Tr...]
    unnamed x2 -> x0, blocking collectives: 129 us -> none
    reduce_sum x17 -> x0, other arithmetic: 39.9 us -> none  [the longest x8 21.2 us: norm_fwd(): return centered * lax.rsqrt(variance + EPS) * gain + shift]
  transfers between devices with their start and end apart: 14 -> 0, of which waited for: 5 -> 0; matrix products, arithmetic and copies ran while one was open for 25% -> 0% of each run, Pallas kernels for 0% -> 0%
where the time goes in v1:
time: 553 us; the launch traced here: 545 us
  Pallas kernels  496 us (90%)
  local copies, waits for them, and re-layouts  42.7 us (8%)
    pallas_call x1, Pallas kernels, scatter_grads(): pl.pallas_call(scatter_kernel, out_shape=[jax.ShapeDtypeStruct(s, F32) fo...  96.8 us
    pallas_call x2, Pallas kernels, attn_bwd(): pl.pallas_call(functools.partial(attn_bwd_kernel, first), grid=(SEQS,), o...  94.7 us
    pallas_call x2, Pallas kernels, attn_fwd(): pl.pallas_call(functools.partial(attn_fwd_kernel, first), grid=(SEQS,), o...  94 us
    pallas_call x1, Pallas kernels, gather_params(): pl.pallas_call(gather_kernel, out_shape=[jax.ShapeDtypeStruct(s, BF16) fo...  92.7 us
    pallas_call x2, Pallas kernels, mlp_bwd(): pl.pallas_call(functools.partial(mlp_bwd_kernel, last), grid=(SEQS,), out...  76.3 us
    pallas_call x2, Pallas kernels, mlp_fwd(): pl.pallas_call(functools.partial(mlp_fwd_kernel, last), grid=(SEQS,), out...  41.1 us
    unnamed x27, local copies, waits for them, and re-layouts  11.9 us

profile of v1, /device:TPU:1, one launch (start us, length us, event | category | flops | bytes accessed | tf_op | source)
XLA Modules:
  0.0 544.8 jit_solution(4427859571993934631)
XLA Ops:
  9.2 1.0 fusion
  10.2 92.7 %gather_params.1 = (bf16[2,4,512,512]{3,2,1,0:T(8,128)(2,1)}, bf16[2,512,2048]{2,1,0:T(8,128)(2,1)}, bf16[2,2048,512]{2,1,0:T(8,128)(2,1)}, bf16[2,4,512,512]{3,...) custom-call(bf16[3,8,16,128]{3,2,1,0:T(8,128)(2,1)} %pad_maximum_fus, ...), custom_call_target="tpu_custom_call" | custom-call | tf_op jit(solution)/shard_map/gather_params/pallas_call | solution.py:669
  103.5 1.7 reduce.3
  106.9 0.9 slice_bitcast_fusion.15
  107.8 2.5 slice_bitcast_fusion.13
  110.3 1.9 slice_bitcast_fusion.9
  112.1 1.4 copy-done.2
  113.6 1.1 slice_bitcast_fusion.11
  114.6 1.9 slice_bitcast_fusion.7
  116.5 1.5 copy-done.7
  118.0 1.5 slice_bitcast_fusion.5.refs_0_
  119.5 1.4 copy-done.6
  120.9 2.4 slice_bitcast_fusion.4
  123.3 1.3 copy-done.5
  124.6 2.7 slice_bitcast_fusion.1
  127.3 1.0 copy-done.4
  128.3 2.3 slice_bitcast_fusion
  130.6 47.2 %attn_fwd.2 = (bf16[4,512,512]{2,1,0:T(8,128)(2,1)}, bf16[4,512,512]{2,1,0:T(8,128)(2,1)}, bf16[4,512,512]{2,1,0:T(8,128)(2,1)}, bf16[4,512,512]{2,1,0:T(8,128)(...) custom-call(s32[4]{0:T(128)} %len_ref.3, bf16[4,512,512]{2,1,0:T(8,128)(2,1)} %x_ref.1, ...), custom_call_target="tpu_custom_call" | custom-call | tf_op jit(solution)/shard_map/attn_fwd/pallas_call | solution.py:267
  177.8 22.5 %mlp_fwd.2 = (bf16[4,512,512]{2,1,0:T(8,128)(2,1)}, bf16[4,2048,512]{2,1,0:T(8,128)(2,1)}, f32[4,2048,512]{2,1,0:T(8,128)}, bf16[4,512,512]{2,1,0:T(8,128)(2,1)}) custom-call(f32[4,512,512]{2,1,0:T(8,128)} %get-tuple-element.57.ctx_ref, bf16[4,512,512]{2,1,0:T(8,128)(2,1)} %get-tuple-element.58.x_ref, bf16[512,512]{1,0:T(8,128)(2,1)} %get-tuple-element.113.wo_ref, ...), custom_call_target="tpu_custom_call" | custom-call | tf_op jit(solution)/shard_map/mlp_fwd/pallas_call | solution.py:278
  200.3 46.7 %attn_fwd.3 = (bf16[4,512,512]{2,1,0:T(8,128)(2,1)}, bf16[4,512,512]{2,1,0:T(8,128)(2,1)}, bf16[4,512,512]{2,1,0:T(8,128)(2,1)}, bf16[4,8,512,512]{3,2,1,0:T(8,128)(2,1)}, f32[4,512,512]{2,1,0:T(8,128)}) custom-call(s32[4]{0:T(128)} %len_ref.3, bf16[4,512,512]{2,1,0:T(8,128)(2,1)} %get-tuple-element.61.x_ref, bf16[3,512,512]{2,1,0:T(8,128)(2,1)} %get-tuple-element.114.w_ref, ...), custom_call_target="tpu_custom_call" | custom-call | tf_op jit(solution)/shard_map/attn_fwd/pallas_call | solution.py:267
  247.0 18.6 %mlp_fwd.3 = (bf16[4,512,512]{2,1,0:T(8,128)(2,1)}, bf16[4,2048,512]{2,1,0:T(8,128)(2,1)}, f32[4,2048,512]{2,1,0:T(8,128)}) custom-call(f32[4,512,512]{2,1,0:T(8,128)} %get-tuple-element.62.ctx_ref, bf16[4,512,512]{2,1,0:T(8,128)(2,1)} %get-tuple-element.61.x_ref, bf16[512,512]{1,0:T(8,128)(2,1)} %get-tuple-element.112.wo_ref, ...), custom_call_target="tpu_custom_call" | custom-call | tf_op jit(solution)/shard_map/mlp_fwd/pallas_call | solution.py:278
  265.6 38.4 %mlp_bwd.2 = (bf16[4,512,512]{2,1,0:T(8,128)(2,1)}, bf16[4,512,512]{2,1,0:T(8,128)(2,1)}, f32[512,512]{1,0:T(8,128)}, f32[512,2048]{1,0:T(8,128)}, f32[2048,512]{1,0:T(8,128)}, /*index=5*/f32[512,128]{1,0:T(8,128)}) custom-call(bf16[4,512,512]{2,1,0:T(8,128)(2,1)} %dy_ref.1, f32[4,2048,512]{2,1,0:T(8,128)} %get-tuple-element.63.slope_ref, ...), custom_call_target="tpu_custom_call" | custom-call | tf_op jit(solution)/shard_map/mlp_bwd/pallas_call | solution.py:287
  304.0 47.3 %attn_bwd.2 = (bf16[4,512,512]{2,1,0:T(8,128)(2,1)}, f32[3,512,512]{2,1,0:T(8,128)}, f32[512,128]{1,0:T(8,128)}) custom-call(bf16[4,512,512]{2,1,0:T(8,128)(2,1)} %get-tuple-element.69.dctx_ref, f32[4,512,512]{2,1,0:T(8,128)} %get-tuple-element.62.ctx_ref, bf16[4,8,512,512]{3,2,1,0:T(8,128)(2,1)} %get-tuple-element.70.p_ref, ...), custom_call_target="tpu_custom_call" | custom-call | tf_op jit(solution)/shard_map/attn_bwd/pallas_call | solution.py:299
  351.3 38.0 %mlp_bwd.3 = (bf16[4,512,512]{2,1,0:T(8,128)(2,1)}, bf16[4,512,512]{2,1,0:T(8,128)(2,1)}, f32[512,512]{1,0:T(8,128)}, f32[512,2048]{1,0:T(8,128)}, f32[2048,512]{1,0:T(8,128)}, /*index=5*/f32[512,128]{1,0:T(8,128)}) custom-call(bf16[4,512,512]{2,1,0:T(8,128)(2,1)} %get-tuple-element.75.dy_ref, f32[4,2048,512]{2,1,0:T(8,128)} %get-tuple-element.76.slope_ref, ...), custom_call_target="tpu_custom_call" | custom-call | tf_op jit(solution)/shard_map/mlp_bwd/pallas_call | solution.py:287
  389.3 47.4 %attn_bwd.3 = (bf16[4,512,512]{2,1,0:T(8,128)(2,1)}, f32[3,512,512]{2,1,0:T(8,128)}, f32[512,128]{1,0:T(8,128)}) custom-call(bf16[4,512,512]{2,1,0:T(8,128)(2,1)} %get-tuple-element.79.dctx_ref, f32[4,512,512]{2,1,0:T(8,128)} %get-tuple-element.57.ctx_ref, bf16[4,8,512,512]{3,2,1,0:T(8,128)(2,1)} %get-tuple-element.80.p_ref, ...), custom_call_target="tpu_custom_call" | custom-call | tf_op jit(solution)/shard_map/attn_bwd/pallas_call | solution.py:299
  436.7 1.1 copy.92
  438.9 96.8 %scatter_grads.1 = (f32[2,4,4,512]{3,2,1,0:T(4,128)}, f32[2,4,2048]{2,1,0:T(4,128)}, f32[2,16,512]{2,1,0:T(8,128)}, f32[32,512]{1,0:T(8,128)}) custom-call(f32[3,4,4,4,8,512]{5,4,3,2,1,0:T(8,128)} %bitcast.89, f32[4,4,4,8,512]{4,3,2,1,0:T(8,128)} %bitcast.94, f32[4,4,4,8,2048]{4,3,2,1,0:T(8,128)} %bitcast.86, f32[4,4,4,4,8,512]{5,4,3,2,1,0:T(8,128)} %bitcast.87, ...), custom_call_target="tpu_custom_call" | custom-call | tf_op jit(solution)/shard_map/scatter_grads/pallas_call | solution.py:762
  535.7 1.3 constant_dynamic-slice_fusion.3
  537.1 1.4 constant_dynamic-slice_fusion
  539.9 1.5 copy.101
  541.4 1.5 copy.102
  542.9 1.5 copy.103
  (55 shorter events, 13.3 us)
Async XLA Ops:
  0.6 2.9 copy-start
  106.6 3.7 copy-start.3
  110.3 3.3 copy-start.2
  114.6 3.3 copy-start.7
  118.0 2.9 copy-start.6
  120.9 3.7 copy-start.5
  124.6 3.7 copy-start.4
  389.3 48.5 %copy-start.10 = (f32[512,128]{1,0:T(8,128)S(1)}, f32[512,128]{1,0:T(8,128)}, u32[]{:S(2)}) copy-start(f32[512,128]{1,0:T(8,128)} %get-tuple-element.94) | copy-start | bytes 786436
  389.3 48.7 %copy-start.9 = (f32[512,128]{1,0:T(8,128)S(1)}, f32[512,128]{1,0:T(8,128)}, u32[]{:S(2)}) copy-start(f32[512,128]{1,0:T(8,128)} %get-tuple-element.97) | copy-start | bytes 786436
  389.3 48.8 %copy-start.8 = (f32[512,128]{1,0:T(8,128)S(1)}, f32[512,128]{1,0:T(8,128)}, u32[]{:S(2)}) copy-start(f32[512,128]{1,0:T(8,128)} %get-tuple-element.96) | copy-start | bytes 786436
  438.9 105.4 %copy-start.1 = (bf16[2,16,512]{2,1,0:T(8,128)(2,1)S(1)}, bf16[2,16,512]{2,1,0:T(8,128)(2,1)}, u32[]{:S(2)}) copy-start(bf16[2,16,512]{2,1,0:T(8,128)(2,1)} %param.24) | copy-start | bytes 98308
